TPU v7x, 32 devices: a whole 2x2x4 slice. The times are simulated.
32 devices in a mesh: tok: 4 (over y, x), din: 4 (over z), dout: 2 (over core).
Axes of the slice: x: 2, y: 2, z: 4, core: 2. Of those that a mesh axis runs over, the one named last changes fastest.
Arguments:
- inputs: bfloat16 [1024, 7168], P(('tok', 'dout'), 'din'), may hold values from -6 to 6
- out_grad: bfloat16 [1024, 9216], P(('tok', 'din'), 'dout'), may hold values from -0.1875 to 0.1875
Outputs:
- weight_grad: bfloat16 [7168, 9216], P(('din', 'tok'), 'dout')
All inputs are finite; a program needn't handle non-finite values.
Results may differ from a plain program's by a relative error of at most 0.014.
Values may be sent and summed in bfloat16 or wider, within the bound.
A program may use at most 64 MiB of HBM per device.

v0:
```python
import jax
import jax.numpy as jnp
from jax import lax
from jax.sharding import PartitionSpec as P


def local(inputs, out_grad):
    gathered = lax.all_gather(inputs, "dout", axis=0, tiled=True)
    partial_term = lax.dot_general(
        gathered,
        lax.all_gather(out_grad, "din", axis=0, tiled=True),
        (((0,), (0,)), ((), ())),
        preferred_element_type=jnp.float32,
    )
    summed = lax.psum_scatter(
        partial_term.astype(jnp.bfloat16), "tok", scatter_dimension=0, tiled=True
    )
    return summed


def solution(mesh):
    placed = (P(("tok", "dout"), "din"), P(("tok", "din"), "dout"))
    return jax.shard_map(
        local, mesh=mesh, in_specs=placed, out_specs=P(("din", "tok"), "dout"), check_vma=False
    )
```

profile of v0, /device:TPU:0, one launch (start us, length us, event | category | flops | bytes accessed | tf_op | source)
XLA Modules:
  0.0 228.7 jit_solution(16414253499212893261)
XLA Ops:
  6.5 0.0 all-gather.2.cloned.1.call-start
  6.5 0.7 all-gather.2.cloned.1.call-update
  7.3 0.0 reduce-scatter.2.cloned.1.call-start
  7.3 2.8 %all_gather.6 = bf16[256,1792]{1,0:T(8,128)(2,1)S(1)} all-gather(bf16[128,1792]{1,0:T(8,128)(2,1)} %param.2), channel_id=1, replica_groups=mesh['tok'=4,'din'=4,'dout'=2] {'dout'}, dimensions={0}, use_global_device_ids=true | all-gather | bytes 1376256 | tf_op jit(solution)/shard_map/all_gather | solution.py:8
  10.1 51.5 %all-gather.2.cloned.1.call-done = bf16[256,4608]{1,0:T(8,128)(2,1)} async-done(((bf16[64,4608]{1,0:T(8,128)(2,1)}), bf16[256,4608]{1,0:T(8,128)(2,1)}) %all-gather.2.cloned.1.call-update) | async-done | bytes 2359312 | tf_op jit(solution)/shard_map/all_gather | solution.py:11
  61.6 9.7 %convolution_convert_fusion = bf16[1792,4608]{1,0:T(8,128)(2,1)} fusion(bf16[256,1792]{1,0:T(8,128)(2,1)S(1)} %all_gather.6, bf16[256,4608]{1,0:T(8,128)(2,1)} %all-gather.2.cloned.1.call-done), kind=kOutput, calls=%fused_computation | convolution fusion | flops 4236115968 | bytes 19791872 | tf_op jit(solution)/shard_map/dot_general | solution.py:9
  71.3 0.0 reduce-scatter.2.cloned.1.call-update
  71.3 150.5 %reduce-scatter.2.cloned.1.call-done = bf16[448,4608]{1,0:T(8,128)(2,1)} async-done(((bf16[1792,4608]{1,0:T(8,128)(2,1)}), bf16[448,4608]{1,0:T(8,128)(2,1)}) %reduce-scatter.2.cloned.1.call-update) | async-done | bytes 4128784 | tf_op jit(solution)/shard_map/reduce_scatter | solution.py:15
Async XLA Ops:
  6.5 55.1 %all-gather.2.cloned.1.call-start = ((), (), s32[]{:S(2)}) async-start(), calls=%async_computation.1 | async-start | bytes 2949120 | tf_op jit(solution)/shard_map/all_gather | solution.py:11
  7.3 214.6 %reduce-scatter.2.cloned.1.call-start = ((), (), s32[]{:S(2)}) async-start(), calls=%async_computation.2 | async-start | bytes 20643840 | tf_op jit(solution)/shard_map/reduce_scatter | solution.py:15
Sparse Core Ops, SparseCore 0:
  8.9 52.6 all-gather.1
  71.4 150.3 reduce-scatter.1
where the time goes:
time: 229 us
  waiting for transfers between devices  203 us (89%)
  between operations  13.4 us (6%)
  matrix products  9.66 us (4%)
  blocking collectives  2.79 us (1%)
    reduce_scatter x1, waiting for transfers between devices, local(): lax.psum_scatter(partial_term.astype(jnp.bfloat16), 'tok', scatter_dimens...  151 us
    all_gather x1, waiting for transfers between devices, local(): lax.all_gather(out_grad, 'din', axis=0, tiled=True)  51.5 us
    dot_general x1, matrix products, local(): lax.dot_general(gathered, lax.all_gather(out_grad, 'din', axis=0, tiled=T...  9.66 us
  transfers between devices with their start and end apart: 2, of which 2 were waited for; matrix products, arithmetic and copies ran while one was open for 0% of the time, Pallas kernels for 0%

commit v1 on v0

v1 whole, which is shorter than its diff:
```python
import functools

import jax
import jax.numpy as jnp
from jax import lax
from jax.experimental import pallas as pl
from jax.experimental.pallas import tpu as pltpu
from jax.sharding import PartitionSpec as P

MESH = pl.DeviceIdType.MESH
LANES = 128
KINDS = 4


def scattered(inputs, out_grad):
    gathered = lax.all_gather(inputs, "dout", axis=0, tiled=True)
    partial_term = lax.dot_general(
        gathered,
        lax.all_gather(out_grad, "din", axis=0, tiled=True),
        (((0,), (0,)), ((), ())),
        preferred_element_type=jnp.float32,
    )
    return lax.psum_scatter(
        partial_term.astype(jnp.bfloat16), "tok", scatter_dimension=0, tiled=True
    )


def kernel(sizes, a_ref, g_ref, o_ref, held, windows, turned, left, made,
           load_sem, a_load, a_send, a_recv, a_pass, a_got, z_send, z_recv, p_send, p_recv, o_sem):
    depth, chunks, rows, window = sizes
    t, z, core = lax.axis_index("tok"), lax.axis_index("din"), lax.axis_index("dout")
    y, x = t // 2, t % 2
    tx, ty = y * 2 + (1 - x), (1 - y) * 2 + x
    td = (1 - y) * 2 + (1 - x)
    wide = KINDS * LANES

    def at_t(other):
        return (other, z, core)

    partner = (t, z, 1 - core)

    def own(c, k):
        return pltpu.make_async_copy(
            g_ref.at[:, pl.ds(pl.multiple_of(c * wide + k * LANES, LANES), LANES)],
            held.at[c, k, y, x, z],
            load_sem.at[c, k],
        )

    def load(c, carry):
        for k in range(KINDS):
            own(c, k).start()
        return carry

    lax.fori_loop(0, chunks, load, 0)

    barrier = pltpu.get_barrier_semaphore()
    for other in (at_t(tx), at_t(ty), at_t(td), partner):
        pl.semaphore_signal(barrier, inc=1, device_id=other, device_id_type=MESH)

    @pl.when(z > 0)
    def _():
        pl.semaphore_signal(barrier, inc=1, device_id=(t, z - 1, core), device_id_type=MESH)

    @pl.when(z < depth - 1)
    def _():
        pl.semaphore_signal(barrier, inc=1, device_id=(t, z + 1, core), device_id_type=MESH)

    pl.semaphore_wait(barrier, 4 + jnp.where(z > 0, 1, 0) + jnp.where(z < depth - 1, 1, 0))

    def slab(owner):
        start = pl.multiple_of((owner * rows) // LANES * LANES, LANES)
        return a_ref.at[:, pl.ds(start, window)]

    def a_copy(j, target):
        return pltpu.make_async_remote_copy(
            src_ref=slab(target), dst_ref=windows.at[t, core],
            send_sem=a_send.at[j], recv_sem=a_recv.at[j],
            device_id=at_t(target), device_id_type=MESH,
        )

    def a_wait(j, source):
        pltpu.make_async_remote_copy(
            src_ref=slab(source), dst_ref=windows.at[source, core],
            send_sem=a_send.at[j], recv_sem=a_recv.at[j],
            device_id=at_t(source), device_id_type=MESH,
        ).wait_recv()

    def a_over(j, source, src):
        return pltpu.make_async_remote_copy(
            src_ref=src, dst_ref=windows.at[source, core],
            send_sem=a_pass.at[j], recv_sem=a_got.at[j],
            device_id=partner, device_id_type=MESH,
        )

    def a_over_wait(j, source):
        pltpu.make_async_remote_copy(
            src_ref=windows.at[source, 1 - core], dst_ref=windows.at[source, 1 - core],
            send_sem=a_pass.at[j], recv_sem=a_got.at[j],
            device_id=partner, device_id_type=MESH,
        ).wait_recv()

    mine = pltpu.make_async_copy(slab(t), windows.at[t, core], a_load)
    mine.start()

    def plane_ref(c, k, last, yy, xx):
        if k == 0:
            return held.at[c, k, yy] if last else held.at[c, k, yy, xx]
        if k == 1:
            return held.at[c, k, :, xx] if last else held.at[c, k, yy, xx]
        if not last:
            return held.at[c, k, yy, xx, z]
        return held.at[c, k, yy] if k == 2 else held.at[c, k, :, xx]

    def along_x(k, last):
        return (k in (0, 2)) != last

    def plane(c, k, last):
        ref = plane_ref(c, k, last, y, x)
        return pltpu.make_async_remote_copy(
            src_ref=ref, dst_ref=ref,
            send_sem=p_send.at[c, k, int(last)], recv_sem=p_recv.at[c, k, int(last)],
            device_id=at_t(tx if along_x(k, last) else ty), device_id_type=MESH,
        )

    def plane_wait(c, k, last):
        yy, xx = (y, 1 - x) if along_x(k, last) else (1 - y, x)
        ref = plane_ref(c, k, last, yy, xx)
        pltpu.make_async_remote_copy(
            src_ref=ref, dst_ref=ref,
            send_sem=p_send.at[c, k, int(last)], recv_sem=p_recv.at[c, k, int(last)],
            device_id=at_t(tx if along_x(k, last) else ty), device_id_type=MESH,
        ).wait_recv()

    def line_ref(c, g, source):
        if g == 0:
            return held.at[c, pl.ds(0, 2), y, x, source]
        return held.at[c, 2, y, :, source] if g == 1 else held.at[c, 3, :, x, source]

    def line(c, g, source, up):
        ref = line_ref(c, g, source)
        return pltpu.make_async_remote_copy(
            src_ref=ref, dst_ref=ref,
            send_sem=z_send.at[c, g, source, up], recv_sem=z_recv.at[c, g, source],
            device_id=(t, z + 1 if up else z - 1, core), device_id_type=MESH,
        )

    def both_ways(c, g):
        @pl.when(z < depth - 1)
        def _():
            line(c, g, z, 1).start()

        @pl.when(z > 0)
        def _():
            line(c, g, z, 0).start()

    def first(c, carry):
        for k in range(KINDS):
            own(c, k).wait()
        for k in (2, 3):
            plane(c, k, False).start()
        return carry

    def send_own(c):
        both_ways(c, 0)
        for k in (2, 3):
            plane_wait(c, k, False)
            both_ways(c, k - 1)

    def pass_on(c):
        for hop in range(1, depth):
            for g in range(3):
                @pl.when(z - hop >= 0)
                def _():
                    line(c, g, z - hop, 0).wait_recv()

                    @pl.when(z < depth - 1)
                    def _():
                        line(c, g, z - hop, 1).start()

                @pl.when(z + hop < depth)
                def _():
                    line(c, g, z + hop, 1).wait_recv()

                    @pl.when(z > 0)
                    def _():
                        line(c, g, z + hop, 0).start()
        for k in (0, 1):
            plane(c, k, False).start()
        for k in (2, 3):
            plane(c, k, True).start()

    def finish(c):
        for k in (0, 1):
            plane_wait(c, k, False)
            plane(c, k, True).start()

    def out_copy(c):
        return pltpu.make_async_copy(
            made.at[c], o_ref.at[:, pl.ds(pl.multiple_of(c * wide, LANES), wide)], o_sem.at[c]
        )

    def multiply(c):
        for k in range(KINDS):
            plane_wait(c, k, True)
        for k in range(0, KINDS, 2):
            pair = [held[c, k + i].reshape(-1, LANES) for i in range(2)]
            term = jnp.dot(
                left[...], jnp.concatenate(pair, axis=1), preferred_element_type=jnp.float32
            )
            made[c, :, k * LANES:(k + 2) * LANES] = term.astype(made.dtype)
        out_copy(c).start()

    first(0, 0)
    for j, target in enumerate((tx, ty, td)):
        a_copy(j, target).start()
    a_over(3, t, slab(t)).start()
    both_ways(0, 0)
    lax.fori_loop(1, chunks, first, 0)
    for k in (2, 3):
        plane_wait(0, k, False)
        both_ways(0, k - 1)

    mine.wait()
    for j, source in enumerate((tx, ty, td)):
        a_wait(j, source)
        a_over(j, source, windows.at[source, core]).start()
    for j, source in enumerate((tx, ty, td, t)):
        a_over_wait(j, source)
    shift = pl.multiple_of((t * rows) % LANES, 16)

    count = windows.shape[0] * 2
    for j in range(count):
        turned[...] = windows[j // 2, j % 2].T
        piece = windows.shape[2]
        left[:, j * piece:(j + 1) * piece] = turned[pl.ds(shift, rows), :]

    def step(i, carry):
        @pl.when(i + 1 < chunks)
        def _():
            send_own(i + 1)

        @pl.when(i < chunks)
        def _():
            pass_on(i)

        @pl.when((i >= 1) & (i < chunks + 1))
        def _():
            finish(i - 1)

        @pl.when(i >= 2)
        def _():
            multiply(i - 2)

        return carry

    lax.fori_loop(0, chunks + 2, step, 0)

    for j, target in enumerate((tx, ty, td)):
        a_copy(j, target).wait_send()
        a_over(j, target, windows.at[target, core]).wait_send()
    a_over(3, t, slab(t)).wait_send()

    def drain(c, carry):
        for k in range(KINDS):
            for last in (False, True):
                plane(c, k, last).wait_send()
        for g in range(3):
            for source in range(depth):
                @pl.when((z < depth - 1) & (z >= source))
                def _():
                    line(c, g, source, 1).wait_send()

                @pl.when((z > 0) & (z <= source))
                def _():
                    line(c, g, source, 0).wait_send()
        out_copy(c).wait()
        return carry

    lax.fori_loop(0, chunks, drain, 0)


def gathered(shape, inputs, out_grad):
    depth = shape["din"]
    groups = shape["tok"]
    rows = inputs.shape[1] // groups
    window = max((j * rows) % LANES for j in range(groups)) + rows
    window = -(-window // LANES) * LANES
    piece = inputs.shape[0]
    tall, columns = out_grad.shape
    wide = KINDS * LANES
    chunks = columns // wide
    tokens = tall * depth * groups
    any_ref = pl.BlockSpec(memory_space=pl.ANY)
    dma = pltpu.SemaphoreType.DMA
    return pl.pallas_call(
        functools.partial(kernel, (depth, chunks, rows, window)),
        out_shape=jax.ShapeDtypeStruct((rows, columns), out_grad.dtype),
        in_specs=[any_ref, any_ref],
        out_specs=any_ref,
        scratch_shapes=[
            pltpu.VMEM((chunks, KINDS, 2, 2, depth, tall, LANES), out_grad.dtype),
            pltpu.VMEM((groups, 2, piece, window), inputs.dtype),
            pltpu.VMEM((window, piece), inputs.dtype),
            pltpu.VMEM((rows, tokens), inputs.dtype),
            pltpu.VMEM((chunks, rows, wide), out_grad.dtype),
            dma((chunks, KINDS)),
            dma,
            dma((3,)),
            dma((3,)),
            dma((4,)),
            dma((4,)),
            dma((chunks, 3, depth, 2)),
            dma((chunks, 3, depth)),
            dma((chunks, KINDS, 2)),
            dma((chunks, KINDS, 2)),
            dma((chunks,)),
        ],
        compiler_params=pltpu.CompilerParams(collective_id=0, has_side_effects=True),
        cost_estimate=pl.CostEstimate(
            flops=2 * rows * tokens * columns,
            bytes_accessed=2 * rows * columns,
            transcendentals=0,
        ),
    )(inputs, out_grad)


def solution(mesh):
    shape = dict(mesh.shape)

    def local(inputs, out_grad):
        groups, depth = shape["tok"], shape["din"]
        rows = inputs.shape[1] // groups
        tall = out_grad.shape[0]
        spread = tall * (groups * depth - 1)
        summed = rows * (groups - 1) + tall * (depth - 1)
        fits = (
            groups == 4
            and shape["dout"] == 2
            and inputs.shape[0] == LANES
            and rows % 16 == 0
            and tall % 16 == 0
            and out_grad.shape[1] % (KINDS * LANES) == 0
        )
        if fits and spread < summed:
            return gathered(shape, inputs, out_grad)
        return scattered(inputs, out_grad)

    placed = (P(("tok", "dout"), "din"), P(("tok", "din"), "dout"))
    return jax.shard_map(
        local, mesh=mesh, in_specs=placed, out_specs=P(("din", "tok"), "dout"), check_vma=False
    )
```

time: 229 us -> 102 us (0.45)
  waiting for transfers between devices: 203 us -> 0 us
  Pallas kernels: 0 us -> 97.7 us
  between operations: 13.4 us -> 0.01 us
  matrix products: 9.66 us -> 0 us
  local copies, waits for them, and re-layouts: 0 us -> 4.42 us
  blocking collectives: 2.79 us -> 0 us
    reduce_scatter x1 -> x0, waiting for transfers between devices: 151 us -> none  [local(): lax.psum_scatter(partial_term.astype(jnp.bfloat16), 'tok', scatter_dimens...]
    pallas_call x0 -> x1, Pallas kernels: none -> 97.7 us  [gathered(): pl.pallas_call(functools.partial(kernel, (depth, chunks, rows, window)),...]
    all_gather x1 -> x0, waiting for transfers between devices: 51.5 us -> none  [local(): lax.all_gather(out_grad, 'din', axis=0, tiled=True)]
    dot_general x1 -> x0, matrix products: 9.66 us -> none  [local(): lax.dot_general(gathered, lax.all_gather(out_grad, 'din', axis=0, tiled=T...]
    unnamed x0 -> x1, local copies, waits for them, and re-layouts: none -> 4.42 us
    all_gather x1 -> x0, blocking collectives: 2.79 us -> none  [local(): gathered = lax.all_gather(inputs, 'dout', axis=0, tiled=True)]
  transfers between devices with their start and end apart: 2 -> 0, of which waited for: 2 -> 0; matrix products, arithmetic and copies ran while one was open for 0% -> 0% of each run, Pallas kernels for 0% -> 0%
where the time goes in v1:
time: 102 us
  Pallas kernels  97.7 us (96%)
  local copies, waits for them, and re-layouts  4.42 us (4%)
    pallas_call x1, Pallas kernels, gathered(): pl.pallas_call(functools.partial(kernel, (depth, chunks, rows, window)),...  97.7 us
    unnamed x1, local copies, waits for them, and re-layouts  4.42 us

profile of v1, /device:TPU:0, one launch (start us, length us, event | category | flops | bytes accessed | tf_op | source)
XLA Modules:
  0.0 102.1 jit_solution(1478917597860319913)
XLA Ops:
  0.0 97.7 %shard_map.28 = bf16[448,4608]{1,0:T(8,128)(2,1)} custom-call(bf16[128,1792]{1,0:T(8,128)(2,1)} %a_ref.1, bf16[64,4608]{1,0:T(8,128)(2,1)} %g_ref.1), custom_call_target="tpu_custom_call" | custom-call | flops 4227858432 | bytes 4128768 | tf_op jit(solution)/shard_map/pallas_call | solution.py:295
  97.7 4.4 %copy.4 = bf16[448,4608]{1,0:T(8,128)(2,1)} copy(bf16[448,4608]{1,0:T(8,128)(2,1)} %shard_map.28) | data formatting | bytes 8257536

commit v2 on v1

--- a/solution.py
+++ b/solution.py
@@ -211,28 +211,29 @@
         out_copy(c).start()
 
     first(0, 0)
+    both_ways(0, 0)
+    lax.fori_loop(1, chunks, first, 0)
     for j, target in enumerate((tx, ty, td)):
         a_copy(j, target).start()
     a_over(3, t, slab(t)).start()
-    both_ways(0, 0)
-    lax.fori_loop(1, chunks, first, 0)
     for k in (2, 3):
         plane_wait(0, k, False)
         both_ways(0, k - 1)
 
-    mine.wait()
-    for j, source in enumerate((tx, ty, td)):
-        a_wait(j, source)
-        a_over(j, source, windows.at[source, core]).start()
-    for j, source in enumerate((tx, ty, td, t)):
-        a_over_wait(j, source)
-    shift = pl.multiple_of((t * rows) % LANES, 16)
-
-    count = windows.shape[0] * 2
-    for j in range(count):
-        turned[...] = windows[j // 2, j % 2].T
+    def share():
+        for j, source in enumerate((tx, ty, td)):
+            a_wait(j, source)
+            a_over(j, source, windows.at[source, core]).start()
+
+    def turn():
+        mine.wait()
+        for j, source in enumerate((tx, ty, td, t)):
+            a_over_wait(j, source)
+        shift = pl.multiple_of((t * rows) % LANES, 16)
         piece = windows.shape[2]
-        left[:, j * piece:(j + 1) * piece] = turned[pl.ds(shift, rows), :]
+        for j in range(windows.shape[0] * 2):
+            turned[...] = windows[j // 2, j % 2].T
+            left[:, j * piece:(j + 1) * piece] = turned[pl.ds(shift, rows), :]
 
     def step(i, carry):
         @pl.when(i + 1 < chunks)
@@ -242,6 +243,14 @@
         @pl.when(i < chunks)
         def _():
             pass_on(i)
+
+        @pl.when(i == 0)
+        def _():
+            share()
+
+        @pl.when(i == 1)
+        def _():
+            turn()
 
         @pl.when((i >= 1) & (i < chunks + 1))
         def _():
@@ -295,7 +304,7 @@
     return pl.pallas_call(
         functools.partial(kernel, (depth, chunks, rows, window)),
         out_shape=jax.ShapeDtypeStruct((rows, columns), out_grad.dtype),
-        in_specs=[any_ref, any_ref],
+        in_specs=[pl.BlockSpec(memory_space=pltpu.HBM)] * 2,
         out_specs=any_ref,
         scratch_shapes=[
             pltpu.VMEM((chunks, KINDS, 2, 2, depth, tall, LANES), out_grad.dtype),
@@ -315,7 +324,9 @@
             dma((chunks, KINDS, 2)),
             dma((chunks,)),
         ],
-        compiler_params=pltpu.CompilerParams(collective_id=0, has_side_effects=True),
+        compiler_params=pltpu.CompilerParams(
+            collective_id=0, has_side_effects=True, vmem_limit_bytes=24 * 2**20
+        ),
         cost_estimate=pl.CostEstimate(
             flops=2 * rows * tokens * columns,
             bytes_accessed=2 * rows * columns,

time: 102 us -> 96.1 us (0.942)
  Pallas kernels: 97.7 us -> 91.8 us
    pallas_call x1, Pallas kernels: 97.7 us -> 91.8 us  [gathered(): pl.pallas_call(functools.partial(kernel, (depth, chunks, rows, window)),...]
    unnamed x1 -> x5, local copies, waits for them, and re-layouts: 4.42 us -> 4.07 us
where the time goes in v2:
time: 96.1 us; the launch traced here: 95.9 us
  Pallas kernels  91.8 us (96%)
  local copies, waits for them, and re-layouts  4.07 us (4%)
    pallas_call x1, Pallas kernels, gathered(): pl.pallas_call(functools.partial(kernel, (depth, chunks, rows, window)),...  91.8 us
    unnamed x5, local copies, waits for them, and re-layouts  4.07 us

profile of v2, /device:TPU:0, one launch (start us, length us, event | category | flops | bytes accessed | tf_op | source)
XLA Modules:
  0.0 95.9 jit_solution(15100700304307813841)
XLA Ops:
  0.0 0.0 copy-start
  0.0 1.1 %copy-done = bf16[64,4608]{1,0:T(8,128)(2,1)S(1)} copy-done((bf16[64,4608]{1,0:T(8,128)(2,1)S(1)}, bf16[64,4608]{1,0:T(8,128)(2,1)}, u32[]{:S(2)}) %copy-start) | copy-done | bytes 589848
  1.1 0.0 copy-start.1
  1.1 1.0 %copy-done.1 = bf16[128,1792]{1,0:T(8,128)(2,1)S(1)} copy-done((bf16[128,1792]{1,0:T(8,128)(2,1)S(1)}, bf16[128,1792]{1,0:T(8,128)(2,1)}, u32[]{:S(2)}) %copy-start.1) | copy-done | bytes 458776
  2.1 91.8 %shard_map.28 = bf16[448,4608]{1,0:T(8,128)(2,1)S(1)} custom-call(bf16[128,1792]{1,0:T(8,128)(2,1)S(1)} %copy-done.1, bf16[64,4608]{1,0:T(8,128)(2,1)S(1)} %copy-done), custom_call_target="tpu_custom_call" | custom-call | flops 4227858432 | bytes 4128768 | tf_op jit(solution)/shard_map/pallas_call | solution.py:304
  93.9 2.0 %copy.4 = bf16[448,4608]{1,0:T(8,128)(2,1)} copy(bf16[448,4608]{1,0:T(8,128)(2,1)S(1)} %shard_map.28) | data formatting | bytes 8257536
Async XLA Ops:
  0.0 1.1 %copy-start = (bf16[64,4608]{1,0:T(8,128)(2,1)S(1)}, bf16[64,4608]{1,0:T(8,128)(2,1)}, u32[]{:S(2)}) copy-start(bf16[64,4608]{1,0:T(8,128)(2,1)} %g_ref.1) | copy-start | bytes 1769476
  1.1 1.0 %copy-start.1 = (bf16[128,1792]{1,0:T(8,128)(2,1)S(1)}, bf16[128,1792]{1,0:T(8,128)(2,1)}, u32[]{:S(2)}) copy-start(bf16[128,1792]{1,0:T(8,128)(2,1)} %a_ref.1) | copy-start | bytes 1376260

commit v3 on v2

--- a/solution.py
+++ b/solution.py
@@ -102,97 +102,150 @@
     mine = pltpu.make_async_copy(slab(t), windows.at[t, core], a_load)
     mine.start()
 
-    def plane_ref(c, k, last, yy, xx):
-        if k == 0:
+    def by_form(c, act):
+        plain = (c > 0) & (c % 3 == 0)
+
+        @pl.when(plain)
+        def _():
+            act(True)
+
+        @pl.when(jnp.logical_not(plain))
+        def _():
+            act(False)
+
+    def order_of(k, plain):
+        return k + 2 if plain and k < 2 else k
+
+    def early(plain):
+        return [k for k in range(KINDS) if order_of(k, plain) < 2]
+
+    def late(plain):
+        return [k for k in range(KINDS) if order_of(k, plain) >= 2]
+
+    def plane_ref(c, k, order, last, yy, xx):
+        if order == 0:
             return held.at[c, k, yy] if last else held.at[c, k, yy, xx]
-        if k == 1:
+        if order == 1:
             return held.at[c, k, :, xx] if last else held.at[c, k, yy, xx]
         if not last:
             return held.at[c, k, yy, xx, z]
-        return held.at[c, k, yy] if k == 2 else held.at[c, k, :, xx]
-
-    def along_x(k, last):
-        return (k in (0, 2)) != last
-
-    def plane(c, k, last):
-        ref = plane_ref(c, k, last, y, x)
+        return held.at[c, k, yy] if order == 2 else held.at[c, k, :, xx]
+
+    def along_x(order, last):
+        return (order in (0, 2)) != last
+
+    def plane_to(c, k, order, last, ref):
         return pltpu.make_async_remote_copy(
             src_ref=ref, dst_ref=ref,
             send_sem=p_send.at[c, k, int(last)], recv_sem=p_recv.at[c, k, int(last)],
-            device_id=at_t(tx if along_x(k, last) else ty), device_id_type=MESH,
-        )
-
-    def plane_wait(c, k, last):
-        yy, xx = (y, 1 - x) if along_x(k, last) else (1 - y, x)
-        ref = plane_ref(c, k, last, yy, xx)
-        pltpu.make_async_remote_copy(
-            src_ref=ref, dst_ref=ref,
-            send_sem=p_send.at[c, k, int(last)], recv_sem=p_recv.at[c, k, int(last)],
-            device_id=at_t(tx if along_x(k, last) else ty), device_id_type=MESH,
-        ).wait_recv()
-
-    def line_ref(c, g, source):
-        if g == 0:
+            device_id=at_t(tx if along_x(order, last) else ty), device_id_type=MESH,
+        )
+
+    def plane(c, k, plain, last):
+        order = order_of(k, plain)
+        return plane_to(c, k, order, last, plane_ref(c, k, order, last, y, x))
+
+    def plane_wait(c, k, plain, last):
+        order = order_of(k, plain)
+        yy, xx = (y, 1 - x) if along_x(order, last) else (1 - y, x)
+        plane_to(c, k, order, last, plane_ref(c, k, order, last, yy, xx)).wait_recv()
+
+    def groups(plain):
+        return late(plain) + ([] if plain else [0])
+
+    def line_ref(c, g, plain, source):
+        order = order_of(g, plain)
+        if order == 0:
             return held.at[c, pl.ds(0, 2), y, x, source]
-        return held.at[c, 2, y, :, source] if g == 1 else held.at[c, 3, :, x, source]
-
-    def line(c, g, source, up):
-        ref = line_ref(c, g, source)
+        return held.at[c, g, y, :, source] if order == 2 else held.at[c, g, :, x, source]
+
+    def line(c, g, plain, source, up):
+        ref = line_ref(c, g, plain, source)
         return pltpu.make_async_remote_copy(
             src_ref=ref, dst_ref=ref,
             send_sem=z_send.at[c, g, source, up], recv_sem=z_recv.at[c, g, source],
             device_id=(t, z + 1 if up else z - 1, core), device_id_type=MESH,
         )
 
-    def both_ways(c, g):
+    def both_ways(c, g, plain):
         @pl.when(z < depth - 1)
         def _():
-            line(c, g, z, 1).start()
+            line(c, g, plain, z, 1).start()
 
         @pl.when(z > 0)
         def _():
-            line(c, g, z, 0).start()
+            line(c, g, plain, z, 0).start()
 
     def first(c, carry):
         for k in range(KINDS):
             own(c, k).wait()
-        for k in (2, 3):
-            plane(c, k, False).start()
+
+        def act(plain):
+            for k in late(plain):
+                plane(c, k, plain, False).start()
+
+        by_form(c, act)
         return carry
 
-    def send_own(c):
-        both_ways(c, 0)
-        for k in (2, 3):
-            plane_wait(c, k, False)
-            both_ways(c, k - 1)
-
-    def pass_on(c):
-        for hop in range(1, depth):
-            for g in range(3):
+    def send_early(c):
+        def act(plain):
+            if not plain:
+                both_ways(c, 0, plain)
+
+        by_form(c, act)
+
+    def send_late(c):
+        def act(plain):
+            for k in late(plain):
+                plane_wait(c, k, plain, False)
+                both_ways(c, k, plain)
+
+        by_form(c, act)
+
+    def pass_on(c, hop):
+        def act(plain):
+            for g in sorted(groups(plain)):
                 @pl.when(z - hop >= 0)
                 def _():
-                    line(c, g, z - hop, 0).wait_recv()
+                    line(c, g, plain, z - hop, 0).wait_recv()
 
                     @pl.when(z < depth - 1)
                     def _():
-                        line(c, g, z - hop, 1).start()
+                        line(c, g, plain, z - hop, 1).start()
 
                 @pl.when(z + hop < depth)
                 def _():
-                    line(c, g, z + hop, 1).wait_recv()
+                    line(c, g, plain, z + hop, 1).wait_recv()
 
                     @pl.when(z > 0)
                     def _():
-                        line(c, g, z + hop, 0).start()
-        for k in (0, 1):
-            plane(c, k, False).start()
-        for k in (2, 3):
-            plane(c, k, True).start()
+                        line(c, g, plain, z + hop, 0).start()
+
+        by_form(c, act)
+
+    def spread(c):
+        def act(plain):
+            for k in early(plain):
+                plane(c, k, plain, False).start()
+            for k in late(plain):
+                plane(c, k, plain, True).start()
+
+        by_form(c, act)
 
     def finish(c):
-        for k in (0, 1):
-            plane_wait(c, k, False)
-            plane(c, k, True).start()
+        def act(plain):
+            for k in early(plain):
+                plane_wait(c, k, plain, False)
+                plane(c, k, plain, True).start()
+
+        by_form(c, act)
+
+    def arrived(c):
+        def act(plain):
+            for k in range(KINDS):
+                plane_wait(c, k, plain, True)
+
+        by_form(c, act)
 
     def out_copy(c):
         return pltpu.make_async_copy(
@@ -200,8 +253,7 @@
         )
 
     def multiply(c):
-        for k in range(KINDS):
-            plane_wait(c, k, True)
+        arrived(c)
         for k in range(0, KINDS, 2):
             pair = [held[c, k + i].reshape(-1, LANES) for i in range(2)]
             term = jnp.dot(
@@ -211,14 +263,17 @@
         out_copy(c).start()
 
     first(0, 0)
-    both_ways(0, 0)
+    send_early(0)
     lax.fori_loop(1, chunks, first, 0)
     for j, target in enumerate((tx, ty, td)):
         a_copy(j, target).start()
     a_over(3, t, slab(t)).start()
-    for k in (2, 3):
-        plane_wait(0, k, False)
-        both_ways(0, k - 1)
+    send_late(0)
+    for c in range(1, depth - 1):
+        for back in range(c):
+            pass_on(back, c - back)
+        send_early(c)
+        send_late(c)
 
     def share():
         for j, source in enumerate((tx, ty, td)):
@@ -236,13 +291,22 @@
             left[:, j * piece:(j + 1) * piece] = turned[pl.ds(shift, rows), :]
 
     def step(i, carry):
-        @pl.when(i + 1 < chunks)
-        def _():
-            send_own(i + 1)
-
         @pl.when(i < chunks)
         def _():
-            pass_on(i)
+            pass_on(i, depth - 1)
+            spread(i)
+
+        for hop in range(depth - 2, 0, -1):
+            ahead = depth - 1 - hop
+
+            @pl.when(i + ahead < chunks)
+            def _():
+                pass_on(i + ahead, hop)
+
+        @pl.when(i + depth - 1 < chunks)
+        def _():
+            send_early(i + depth - 1)
+            send_late(i + depth - 1)
 
         @pl.when(i == 0)
         def _():
@@ -270,18 +334,21 @@
     a_over(3, t, slab(t)).wait_send()
 
     def drain(c, carry):
-        for k in range(KINDS):
-            for last in (False, True):
-                plane(c, k, last).wait_send()
-        for g in range(3):
-            for source in range(depth):
-                @pl.when((z < depth - 1) & (z >= source))
-                def _():
-                    line(c, g, source, 1).wait_send()
-
-                @pl.when((z > 0) & (z <= source))
-                def _():
-                    line(c, g, source, 0).wait_send()
+        def act(plain):
+            for k in range(KINDS):
+                for last in (False, True):
+                    plane(c, k, plain, last).wait_send()
+            for g in groups(plain):
+                for source in range(depth):
+                    @pl.when((z < depth - 1) & (z >= source))
+                    def _():
+                        line(c, g, plain, source, 1).wait_send()
+
+                    @pl.when((z > 0) & (z <= source))
+                    def _():
+                        line(c, g, plain, source, 0).wait_send()
+
+        by_form(c, act)
         out_copy(c).wait()
         return carry
 
@@ -318,8 +385,8 @@
             dma((3,)),
             dma((4,)),
             dma((4,)),
-            dma((chunks, 3, depth, 2)),
-            dma((chunks, 3, depth)),
+            dma((chunks, KINDS, depth, 2)),
+            dma((chunks, KINDS, depth)),
             dma((chunks, KINDS, 2)),
             dma((chunks, KINDS, 2)),
             dma((chunks,)),

time: 96.1 us -> 94.9 us (0.988)
  Pallas kernels: 91.8 us -> 90.6 us
    pallas_call x1, Pallas kernels: 91.8 us -> 90.6 us  [gathered(): pl.pallas_call(functools.partial(kernel, (depth, chunks, rows, window)),...]
where the time goes in v3:
time: 94.9 us; the launch traced here: 94.7 us
  Pallas kernels  90.6 us (95%)
  local copies, waits for them, and re-layouts  4.07 us (4%)
    pallas_call x1, Pallas kernels, gathered(): pl.pallas_call(functools.partial(kernel, (depth, chunks, rows, window)),...  90.6 us
    unnamed x5, local copies, waits for them, and re-layouts  4.07 us

profile of v3, /device:TPU:0, one launch (start us, length us, event | category | flops | bytes accessed | tf_op | source)
XLA Modules:
  0.0 94.7 jit_solution(14721599299373535264)
XLA Ops:
  0.0 0.0 copy-start
  0.0 1.1 %copy-done = bf16[64,4608]{1,0:T(8,128)(2,1)S(1)} copy-done((bf16[64,4608]{1,0:T(8,128)(2,1)S(1)}, bf16[64,4608]{1,0:T(8,128)(2,1)}, u32[]{:S(2)}) %copy-start) | copy-done | bytes 589848
  1.1 0.0 copy-start.1
  1.1 1.0 %copy-done.1 = bf16[128,1792]{1,0:T(8,128)(2,1)S(1)} copy-done((bf16[128,1792]{1,0:T(8,128)(2,1)S(1)}, bf16[128,1792]{1,0:T(8,128)(2,1)}, u32[]{:S(2)}) %copy-start.1) | copy-done | bytes 458776
  2.1 90.6 %shard_map.28 = bf16[448,4608]{1,0:T(8,128)(2,1)S(1)} custom-call(bf16[128,1792]{1,0:T(8,128)(2,1)S(1)} %copy-done.1, bf16[64,4608]{1,0:T(8,128)(2,1)S(1)} %copy-done), custom_call_target="tpu_custom_call" | custom-call | flops 4227858432 | bytes 4128768 | tf_op jit(solution)/shard_map/pallas_call | solution.py:371
  92.7 2.0 %copy.4 = bf16[448,4608]{1,0:T(8,128)(2,1)} copy(bf16[448,4608]{1,0:T(8,128)(2,1)S(1)} %shard_map.28) | data formatting | bytes 8257536
Async XLA Ops:
  0.0 1.1 %copy-start = (bf16[64,4608]{1,0:T(8,128)(2,1)S(1)}, bf16[64,4608]{1,0:T(8,128)(2,1)}, u32[]{:S(2)}) copy-start(bf16[64,4608]{1,0:T(8,128)(2,1)} %g_ref.1) | copy-start | bytes 1769476
  1.1 1.0 %copy-start.1 = (bf16[128,1792]{1,0:T(8,128)(2,1)S(1)}, bf16[128,1792]{1,0:T(8,128)(2,1)}, u32[]{:S(2)}) copy-start(bf16[128,1792]{1,0:T(8,128)(2,1)} %a_ref.1) | copy-start | bytes 1376260
